TPU v7x, 128 devices: a whole 4x4x4 slice. The times are simulated.
128 devices in a mesh: blk: 16 (over z_lo, y, core), seq: 8 (over x, z_hi).
Axes of the slice: x: 4, y: 4, z: 4 (z_hi: 2, z_lo: 2; z = z_hi * 2 + z_lo), core: 2. Of those that a mesh axis runs over, the one named last changes fastest.
Arguments:
- layer_input: bfloat16 [16, 1024, 8192], P('blk', 'seq'), may hold values from -6 to 6
- queries: bfloat16 [16, 1024, 4096], P('blk', 'seq'), may hold values from -48 to 48, as said below
- grad_out: bfloat16 [16, 1024, 4096], P('blk', 'seq'), may hold values from -6 to 6
- segment_ids: int32 [16, 1024], P('blk', 'seq'), may hold values from 0 to 3, never falling along the last dimension, each value on 1 to 512 neighbouring positions
- kv_weight: bfloat16 [8192, 1024], P(('blk', 'seq')), may hold values from -0.0625 to 0.0625
- norm_gain: float32 [8192], replicated, may hold values from 0.5 to 1.5
Outputs:
- attended: bfloat16 [16, 1024, 4096], P('blk', 'seq')
- grad_queries: bfloat16 [16, 1024, 4096], P('blk', 'seq')
- grad_input: bfloat16 [16, 1024, 8192], P('blk', 'seq')
- grad_weight: float32 [8192, 1024], P(('blk', 'seq'))
- grad_gain: float32 [8192], replicated
Inputs may be any that keep to these rules, and one draw needn't show every extreme that they name: Projected queries; some rows may be larger than others.
All inputs are finite; a program needn't handle non-finite values.
Results may differ from a plain program's by a relative error of at most 0.02.
The roundings to bfloat16 on the way count: a program that leaves them out, or rounds other values in their place, can miss the bound.
Values may be sent and summed in bfloat16 or wider, within the bound.
No kernel may reach another device: no remote copies, remote signals or barrier semaphores. Data moves between devices by JAX's collectives and lax.ppermute only.
A program may use at most 128 MiB of HBM per device.

v0:
```python
import jax
import jax.numpy as jnp
from jax import lax
from jax.sharding import PartitionSpec as P

HEAD = 128
epsilon = 1e-05


def cut_along(shard, dim, length):
    lengths = shard.shape
    pieces = shard.reshape(*lengths[:dim], length, lengths[dim] // length, *lengths[dim + 1 :])
    return jnp.moveaxis(pieces, dim, 0)


def sum_at_owner(shard, axis, dim):
    length = lax.axis_size(axis)
    pieces = lax.all_to_all(cut_along(shard, dim, length), axis, 0, 0, tiled=True)
    return jnp.sum(pieces, axis=0)


def shards(layer_input, queries, grad_out, segment_ids, kv_weight, norm_gain):
    f32 = jnp.float32
    tok_rows = layer_input.shape[1]
    model_width = layer_input.shape[2]
    seq_devices = lax.axis_size("seq")
    blk_devices = lax.axis_size("blk")
    length = tok_rows * seq_devices
    seq_index = lax.axis_index("seq")
    kv_total = kv_weight.shape[1]
    kv_width = kv_total // 2
    kv_heads = kv_width // HEAD
    query_count = queries.shape[2] // HEAD
    group_size = query_count // kv_heads
    score_scale = HEAD ** (-0.5)
    piece_cols = kv_weight.shape[0]
    source = layer_input[0].astype(f32)
    inv_rms = lax.rsqrt(jnp.mean(source * source, axis=1, keepdims=True) + epsilon)
    scaled = source * inv_rms
    normed = (scaled * norm_gain).astype(jnp.bfloat16)
    split_cols = normed.reshape(tok_rows, blk_devices, seq_devices, piece_cols)
    columns = lax.all_to_all(split_cols, "seq", split_axis=2, concat_axis=0, tiled=True).reshape(
        length, blk_devices * piece_cols
    )
    weight_slab = lax.all_gather(kv_weight, "blk", axis=0, tiled=True)
    query_heads = queries[0].reshape(tok_rows, kv_heads, group_size, HEAD)
    query_pos = seq_index * tok_rows + jnp.arange(tok_rows, dtype=jnp.int32)
    query_doc = segment_ids[0]
    grad_heads = grad_out[0].reshape(tok_rows, kv_heads, group_size, HEAD).transpose(1, 2, 0, 3)

    def scores_of(kv_piece, doc_piece):
        rows_here = kv_piece.shape[0]
        key_heads = kv_piece[:, :kv_width].reshape(rows_here, kv_heads, HEAD)
        raw_scores = (
            jnp.einsum("qgjd,kgd->gjqk", query_heads, key_heads, preferred_element_type=f32)
            * score_scale
        )
        key_pos = jnp.arange(rows_here, dtype=jnp.int32)
        allowed = (key_pos[None, :] <= query_pos[:, None]) & (
            doc_piece[None, :] == query_doc[:, None]
        )
        return (jnp.where(allowed, raw_scores, -1e30), allowed, key_heads)

    stat_shape = (kv_heads, group_size, tok_rows, 1)
    kv_own = sum_at_owner(
        jnp.dot(columns, weight_slab, preferred_element_type=f32), "seq", 0
    ).astype(jnp.bfloat16)
    row_max = jnp.full(stat_shape, -1e30, f32)
    kv_piece = lax.all_gather(kv_own, "seq", axis=0, tiled=True)
    doc_piece = lax.all_gather(query_doc, "seq", axis=0, tiled=True)
    rows_here = kv_piece.shape[0]
    masked, allowed, key_heads = scores_of(kv_piece, doc_piece)
    new_max = jnp.maximum(row_max, jnp.max(masked, axis=-1, keepdims=True))
    expo_terms = jnp.where(allowed, jnp.exp(masked - new_max), 0.0)
    value_heads = kv_piece[:, kv_width:].reshape(rows_here, kv_heads, HEAD)
    weights = expo_terms.astype(jnp.bfloat16)
    weighted = jnp.einsum("gjqk,kgd->gjqd", weights, value_heads, preferred_element_type=f32)
    row_sum = jnp.sum(expo_terms, axis=-1, keepdims=True)
    row_max, row_sum, weighted = (new_max, row_sum, weighted)
    summed = weighted / row_sum
    attended = (
        summed.transpose(2, 0, 1, 3).reshape(tok_rows, query_count * HEAD).astype(jnp.bfloat16)
    )
    log_total = row_max + jnp.log(row_sum)
    attended_heads = attended.reshape(tok_rows, kv_heads, group_size, HEAD).transpose(1, 2, 0, 3)
    row_delta = jnp.sum(grad_heads.astype(f32) * attended_heads.astype(f32), axis=-1, keepdims=True)
    kv_piece = lax.all_gather(kv_own, "seq", axis=0, tiled=True)
    doc_piece = lax.all_gather(query_doc, "seq", axis=0, tiled=True)
    rows_here = kv_piece.shape[0]
    masked, allowed, key_heads = scores_of(kv_piece, doc_piece)
    softmax_probs = jnp.where(allowed, jnp.exp(masked - log_total), 0.0)
    value_heads = kv_piece[:, kv_width:].reshape(rows_here, kv_heads, HEAD)
    grad_probs = jnp.einsum("gjqd,kgd->gjqk", grad_heads, value_heads, preferred_element_type=f32)
    grad_scores = (softmax_probs * (grad_probs - row_delta)).astype(jnp.bfloat16)
    probs_half = softmax_probs.astype(jnp.bfloat16)
    grad_values = jnp.einsum("gjqk,gjqd->kgd", probs_half, grad_heads, preferred_element_type=f32)
    grad_keys = (
        jnp.einsum("gjqk,qgjd->kgd", grad_scores, query_heads, preferred_element_type=f32)
        * score_scale
    )
    grad_query = (
        jnp.einsum("gjqk,kgd->qgjd", grad_scores, key_heads, preferred_element_type=f32)
        * score_scale
    )
    new_rows = jnp.concatenate(
        [grad_keys.reshape(rows_here, kv_width), grad_values.reshape(rows_here, kv_width)], axis=1
    )
    grad_rows = new_rows
    grad_query, grad_rows = (grad_query, grad_rows)
    grad_own = sum_at_owner(grad_rows, "seq", 0).astype(jnp.bfloat16)
    grad_kv = lax.all_gather(grad_own, "seq", axis=0, tiled=True)
    grad_queries = grad_query.reshape(tok_rows, query_count * HEAD).astype(jnp.bfloat16)
    slab_back = lax.all_gather(kv_weight, "blk", axis=0, tiled=True)
    grad_weight = lax.psum_scatter(
        lax.dot_general(columns, grad_kv, (((0,), (0,)), ((), ())), preferred_element_type=f32),
        "blk",
        scatter_dimension=0,
        tiled=True,
    )
    grad_cols = lax.dot_general(
        grad_kv, slab_back, (((1,), (1,)), ((), ())), preferred_element_type=f32
    ).astype(jnp.bfloat16)
    grad_cols = grad_cols.reshape(length, blk_devices, 1, piece_cols)
    grad_normed = lax.all_to_all(grad_cols, "seq", split_axis=0, concat_axis=2, tiled=True).reshape(
        tok_rows, model_width
    )
    grad_norm = grad_normed.astype(f32)
    grad_gain = lax.psum(jnp.sum(grad_norm * scaled, axis=0), ("blk", "seq"))
    grad_hat = grad_norm * norm_gain
    grad_input = inv_rms * (grad_hat - scaled * jnp.mean(grad_hat * scaled, axis=1, keepdims=True))
    return (
        attended[None],
        grad_queries[None],
        grad_input.astype(jnp.bfloat16)[None],
        grad_weight,
        grad_gain,
    )


def solution(mesh):
    in_specs = (
        P("blk", "seq", None),
        P("blk", "seq", None),
        P("blk", "seq", None),
        P("blk", "seq"),
        P(("blk", "seq"), None),
        P(),
    )
    out_specs = (
        P("blk", "seq", None),
        P("blk", "seq", None),
        P("blk", "seq", None),
        P(("blk", "seq"), None),
        P(),
    )
    return jax.shard_map(shards, mesh=mesh, in_specs=in_specs, out_specs=out_specs, check_vma=False)
```

profile of v0, /device:TPU:1, one launch (start us, length us, event | category | flops | bytes accessed | tf_op | source)
XLA Modules:
  0.0 534.6 jit_solution(473694179402004484)
XLA Ops:
  8.0 3.2 copy.148
  17.7 38.3 %all_to_all.34 = bf16[128,16,8,64]{0,3,1,2:T(8,128)(2,1)} all-to-all(bf16[128,16,8,64]{0,3,1,2:T(8,128)(2,1)S(1)} %copy.149), channel_id=1, replica_groups=mesh['blk'=16,'seq'=8] {'seq'}, dimensions={2} | all-to-all | bytes 4194304 | tf_op jit(solution)/shard_map/all_to_all | solution.py:42
  56.0 8.3 %all-gather.5.cloned.1.call-done = bf16[1024,1024]{1,0:T(8,128)(2,1)} async-done(((bf16[64,1024]{1,0:T(8,128)(2,1)}), bf16[1024,1024]{1,0:T(8,128)(2,1)}) %all-gather.5.cloned.1.call-update) | async-done | bytes 2097168 | tf_op jit(solution)/shard_map/all_gather | solution.py:45
  64.3 4.6 fusion.22
  68.9 55.1 %all_to_all.35 = f32[8,128,1024]{2,1,0:T(8,128)} all-to-all(f32[8,128,1024]{2,1,0:T(8,128)S(1)} %fusion.22), channel_id=1, replica_groups=mesh['blk'=16,'seq'=8] {'seq'}, dimensions={0} | all-to-all | bytes 8388608 | tf_op jit(solution)/shard_map/all_to_all | solution.py:18
  124.1 3.4 reduce_sum.66
  131.0 17.1 %all-gather = s32[1,1024]{1,0:T(1,128)S(1)} all-gather(s32[1,128]{1,0:T(1,128)S(1)} %copy-done.8), channel_id=2, replica_groups=mesh['blk'=16,'seq'=8] {'seq'}, dimensions={1}, use_global_device_ids=true | all-gather | bytes 4608 | tf_op jit(solution)/shard_map/all_gather | solution.py:70
  148.4 30.2 %all-gather.7.cloned.1.call-done = bf16[1024,1024]{1,0:T(8,128)(2,1)} async-done(((bf16[128,1024]{1,0:T(8,128)(2,1)}), bf16[1024,1024]{1,0:T(8,128)(2,1)}) %all-gather.7.cloned.1.call-update) | async-done | bytes 2097168 | tf_op jit(solution)/shard_map/all_gather | solution.py:69
  183.0 9.1 %fusion.33 = (f32[4,8,128]{2,1,0:T(8,128)S(1)}, f32[4,8,128,1024]{2,3,1,0:T(8,128)}) fusion(bf16[1024,4,128,1]{0,2,3,1:T(8,128)(2,1)S(1)} %bitcast.122, bf16[128,4,8,128]{3,2,1,0:T(8,128)(2,1)} %bitcast.124, pred[128,1024]{0,1:T(8,128)(4,1)S(1)} %fusion.29), kind=kOutput, calls=%fused_computation.52 | convolution fusion | flops 1086320640 | bytes 19021824 | tf_op jit(solution)/shard_map/qgjd,kgd->gjqk/dot_general | solution.py:55
  194.4 8.7 %fusion.1 = f32[4,8,128]{2,1,0:T(8,128)S(1)} fusion(f32[4,8,128,1024]{2,3,1,0:T(8,128)} %get-tuple-element.45, f32[4,8,128]{2,1,0:T(8,128)S(1)} %broadcast_maximum_fusion, pred[128,1024]{0,1:T(8,128)(4,1)S(1)} %fusion.29), kind=kLoop, calls=%fused_computation.5 | loop fusion | flops 12578816 | bytes 16941056 | tf_op jit(solution)/shard_map/reduce_sum | solution.py:78
  203.1 9.9 %fusion.21 = (bf16[128,4,8,128]{0,3,2,1:T(8,128)(2,1)}, f32[4,8,128,128]{2,3,1,0:T(8,128)S(1)}) fusion(f32[128,4,8]{0,2,1:T(8,128)S(1)} %bitcast.140, bf16[1024,4,128,1]{0,2,3,1:T(8,128)(2,1)S(1)} %bitcast.138, f32[4,8,128,1024]{2,3,1,0:T(8,128)} %get-tuple-element.45, f32[4,8,128]{2,1,0:T(8,128)S(1)} %broadcast_maximum_fusion, ...), kind=kOutput, calls=%fused_computation.32 | convolution fusion | flops 1087373312 | bytes 21135360 | tf_op jit(solution)/shard_map/gjqk,kgd->gjqd/dot_general | solution.py:77
  213.4 9.5 %fusion.24 = f32[1024,4,128]{2,0,1:T(8,128)} fusion(bf16[4,8,128,128]{2,3,1,0:T(8,128)(2,1)S(1)} %bitcast.131, f32[4,8,128,1024]{2,3,1,0:T(8,128)} %get-tuple-element.45, f32[4,8,128]{2,1,0:T(8,128)S(1)} %log_add_fusion, pred[128,1024]{0,1:T(8,128)(4,1)S(1)} %fusion.29), kind=kOutput, calls=%fused_computation.39 | convolution fusion | flops 1086324736 | bytes 20070400 | tf_op jit(solution)/shard_map/gjqk,gjqd->kgd/dot_general | solution.py:96
  222.9 10.9 %fusion = bf16[4,8,128,1024]{2,3,1,0:T(8,128)(2,1)} fusion(f32[4,8,128,1024]{2,3,1,0:T(8,128)} %get-tuple-element.45, bf16[1024,4,128,1]{0,2,3,1:T(8,128)(2,1)S(1)} %bitcast.139, bf16[4,8,128,128]{2,3,1,0:T(8,128)(2,1)S(1)} %bitcast.132, f32[4,8,128]{2,1,0:T(8,128)S(1)} %multiply_reduce_fusion.3, f32[4,8,128]{2,1,0:T(8,128)S(1)} %log_add_fusion, ...), kind=kOutput, calls=%fused_computation.1 | convolution fusion | flops 1094713344 | bytes 27426816 | tf_op jit(solution)/shard_map/gjqd,kgd->gjqk/dot_general | solution.py:93
  236.7 3.5 copy.194
  240.2 7.1 %fusion.20 = f32[1024,4,128]{2,0,1:T(8,128)} fusion(bf16[4,8,128,1024]{2,3,1,0:T(8,128)(2,1)} %fusion, bf16[128,4,8,128]{3,2,1,0:T(8,128)(2,1)S(1)} %bitcast.125), kind=kOutput, calls=%fused_computation.30 | convolution fusion | flops 1074266112 | bytes 11534336 | tf_op jit(solution)/shard_map/gjqk,qgjd->kgd/dot_general | solution.py:98
  253.5 50.9 %all_to_all.36 = f32[8,128,1024]{1,2,0:T(8,128)} all-to-all(f32[8,128,1024]{1,2,0:T(8,128)S(1)} %copy.164), channel_id=1, replica_groups=mesh['blk'=16,'seq'=8] {'seq'}, dimensions={0} | all-to-all | bytes 8388608 | tf_op jit(solution)/shard_map/all_to_all | solution.py:18
  304.4 3.2 reduce_sum.69
  307.8 4.7 copy.171
  312.5 51.4 %all-gather.9.cloned.1.call-done = bf16[1024,1024]{0,1:T(8,128)(2,1)} async-done(((bf16[128,1024]{0,1:T(8,128)(2,1)}), bf16[1024,1024]{0,1:T(8,128)(2,1)}) %all-gather.9.cloned.1.call-update) | async-done | bytes 2097168 | tf_op jit(solution)/shard_map/all_gather | solution.py:111
  363.9 6.5 %fusion.17 = f32[1024,1024]{1,0:T(8,128)} fusion(bf16[1024,1024]{0,1:T(8,128)(2,1)} %all-gather.9.cloned.1.call-done, bf16[128,8,8,128]{3,2,1,0:T(8,128)(2,1)} %bitcast.135), kind=kOutput, calls=%fused_computation.26 | convolution fusion | flops 2147483648 | bytes 8388608 | tf_op jit(solution)/shard_map/dot_general | solution.py:115
  370.4 5.9 %convolution_convert_fusion = bf16[1024,1024]{0,1:T(8,128)(2,1)} fusion(bf16[1024,1024]{1,0:T(8,128)(2,1)} %all-gather.5.cloned.1.call-done, bf16[1024,1024]{0,1:T(8,128)(2,1)} %all-gather.9.cloned.1.call-done), kind=kOutput, calls=%fused_computation.38 | convolution fusion | flops 2148532224 | bytes 6291456 | tf_op jit(solution)/shard_map/dot_general | solution.py:120
  376.3 6.2 %copy.166 = bf16[1024,16,1,64]{3,1,2,0:T(8,128)(2,1)} copy(bf16[1024,16,1,64]{0,3,1,2:T(8,128)(2,1)} %bitcast.134) | data formatting | bytes 4194304 | tf_op jit(solution)/shard_map/reshape | solution.py:123
  382.5 7.6 %reshape.223 = bf16[8,2,65536]{2,1,0:T(2,128)(2,1)} reshape(bf16[1024,1,16,64]{3,2,1,0:T(8,128)(2,1)} %bitcast.119) | data formatting | bytes 4194304
  390.1 4.6 all-to-all-start.3
  397.9 5.6 %multiply_convert_fusion.1 = bf16[4,128,8,128]{3,1,2,0:T(8,128)(2,1)} fusion(bf16[1024,4,128,1]{0,2,3,1:T(8,128)(2,1)S(1)} %bitcast.123, bf16[4,8,128,1024]{2,3,1,0:T(8,128)(2,1)} %fusion), kind=kOutput, calls=%fused_computation.35 | convolution fusion | flops 1074790400 | bytes 10485760 | tf_op jit(solution)/shard_map/gjqk,kgd->qgjd/dot_general | solution.py:102
  405.9 22.6 %all-to-all-done.3 = bf16[8,2,65536]{2,1,0:T(2,128)(2,1)} async-done(((bf16[8,2,65536]{2,1,0:T(2,128)(2,1)}), bf16[8,2,65536]{2,1,0:T(2,128)(2,1)}, u32[]{:S(2)}, u32[]{:S(2)}) %all-to-all-start.3) | async-done | bytes 2097184 | tf_op jit(solution)/shard_map/all_to_all | solution.py:124
  428.4 7.4 %reshape.224 = bf16[1024,1,16,64]{3,2,1,0:T(8,128)(2,1)} reshape(bf16[8,2,65536]{2,1,0:T(2,128)(2,1)} %all-to-all-done.3) | data formatting | bytes 4194304
  435.8 5.5 %copy.167 = bf16[1024,16,1,64]{0,3,2,1:T(8,128)(2,1)} copy(bf16[1024,16,1,64]{3,1,2,0:T(8,128)(2,1)} %bitcast.120) | data formatting | bytes 4194304 | tf_op jit(solution)/shard_map/all_to_all | solution.py:124
  446.7 4.8 multiply_reduce_fusion
  451.5 4.4 fusion.16
  455.9 4.1 copy.175
  460.2 67.6 %psum.7 = f32[8192]{0:T(1024)} all-reduce(f32[8192]{0:T(1024)S(1)} %reduce_sum.72), channel_id=1, replica_groups=mesh['blk'=16,'seq'=8] {'blk','seq'}, use_global_device_ids=true, to_apply=%region_9.10 | all-reduce | flops 8192 | bytes 65536 | tf_op jit(solution)/shard_map/psum | solution.py:128
  (57 shorter events, 38.8 us)
Async XLA Ops:
  7.2 57.1 %all-gather.5.cloned.1.call-start = ((), (), s32[]{:S(2)}) async-start(), calls=%async_computation.5 | async-start | bytes 2228224 | tf_op jit(solution)/shard_map/all_gather | solution.py:45
  7.9 5.5 %copy-start.7 = (f32[8192]{0:T(1024)S(1)}, f32[8192]{0:T(1024)}, u32[]{:S(2)}) copy-start(f32[8192]{0:T(1024)} %param.11) | copy-start | bytes 98308
  7.9 170.6 %all-gather.7.cloned.1.call-start = ((), (), s32[]{:S(2)}) async-start(), calls=%async_computation.6 | async-start | bytes 2359296 | tf_op jit(solution)/shard_map/all_gather | solution.py:69
  124.0 3.5 copy-start.5
  124.0 7.0 %copy-start.8 = (s32[1,128]{1,0:T(1,128)S(1)}, s32[1,128]{1,0:T(1,128)}, u32[]{:S(2)}) copy-start(s32[1,128]{1,0:T(1,128)} %param.9) | copy-start | bytes 1540
  127.5 236.4 %all-gather.9.cloned.1.call-start = ((), (), s32[]{:S(2)}) async-start(), calls=%async_computation.7 | async-start | bytes 2359296 | tf_op jit(solution)/shard_map/all_gather | solution.py:111
  194.4 8.7 %copy-start.6 = (bf16[1024,512]{0,1:T(8,128)(2,1)S(1)}, bf16[1024,512]{0,1:T(8,128)(2,1)}, u32[]{:S(2)}) copy-start(bf16[1024,512]{0,1:T(8,128)(2,1)} %copy.154) | copy-start | bytes 3145732
  203.1 9.9 %copy-start.3 = (bf16[1,128,4096]{1,2,0:T(8,128)(2,1)S(1)}, bf16[1,128,4096]{1,2,0:T(8,128)(2,1)}, u32[]{:S(2)}) copy-start(bf16[1,128,4096]{1,2,0:T(8,128)(2,1)} %copy.156) | copy-start | bytes 3145732
  236.7 3.5 copy-start.1
  250.2 2.2 copy-start.2
  307.6 220.3 %reduce-scatter.2.cloned.1.call-start = ((), (), s32[]{:S(2)}) async-start(), calls=%async_computation.8 | async-start | bytes 4456448 | tf_op jit(solution)/shard_map/reduce_scatter | solution.py:114
  390.1 38.4 %all-to-all-start.3 = ((bf16[8,2,65536]{2,1,0:T(2,128)(2,1)}), bf16[8,2,65536]{2,1,0:T(2,128)(2,1)}, u32[]{:S(2)}, u32[]{:S(2)}) async-start(bf16[8,2,65536]{2,1,0:T(2,128)(2,1)} %reshape.223), calls=%async_computation.3 | async-start | bytes 4194304 | tf_op jit(solution)/shard_map/all_to_all | solution.py:124
  444.4 2.2 copy-start
  444.4 2.3 copy-start.4
Sparse Core Ops, SparseCore 0:
  9.7 54.5 all-gather.4
  127.6 50.8 all-gather.6
  307.7 56.0 all-gather.8
  370.5 72.2 reduce-scatter.1
where the time goes:
time: 540 us; the launch traced here: 535 us
  blocking collectives  229 us (42%)
  waiting for transfers between devices  113 us (21%)
  local copies, waits for them, and re-layouts  70.6 us (13%)
  matrix products  69.1 us (13%)
  other arithmetic  33.7 us (6%)
  between operations  14.2 us (3%)
    all_to_all x2, blocking collectives, sum_at_owner(): lax.all_to_all(cut_along(shard, dim, length), axis, 0, 0, tiled=True)  106 us
    psum x1, blocking collectives, shards(): grad_gain = lax.psum(jnp.sum(grad_norm * scaled, axis=0), ('blk', 'seq'))  67.6 us
    all_gather x1, waiting for transfers between devices, shards(): grad_kv = lax.all_gather(grad_own, 'seq', axis=0, tiled=True)  51.4 us
    unnamed x29, local copies, waits for them, and re-layouts  38.6 us
    all_to_all x1, blocking collectives, shards(): lax.all_to_all(split_cols, 'seq', split_axis=2, concat_axis=0, tiled=True)  38.3 us
    all_gather x1, waiting for transfers between devices, shards(): kv_piece = lax.all_gather(kv_own, 'seq', axis=0, tiled=True)  30.2 us
    all_to_all x1, waiting for transfers between devices, shards(): lax.all_to_all(grad_cols, 'seq', split_axis=0, concat_axis=2, tiled=True)  22.6 us
    all_gather x1, blocking collectives, shards(): doc_piece = lax.all_gather(query_doc, 'seq', axis=0, tiled=True)  17.1 us
  transfers between devices with their start and end apart: 5, of which 4 were waited for; matrix products, arithmetic and copies ran while one was open for 15% of the time, Pallas kernels for 0%

commit v1 on v0

--- a/solution.py
+++ b/solution.py
@@ -108,7 +108,9 @@
     grad_rows = new_rows
     grad_query, grad_rows = (grad_query, grad_rows)
     grad_own = sum_at_owner(grad_rows, "seq", 0).astype(jnp.bfloat16)
-    grad_kv = lax.all_gather(grad_own, "seq", axis=0, tiled=True)
+    grad_kv = jnp.concatenate(
+        lax.all_to_all(jnp.stack([grad_own] * lax.axis_size("seq")), "seq", 0, 0), axis=0
+    )
     grad_queries = grad_query.reshape(tok_rows, query_count * HEAD).astype(jnp.bfloat16)
     slab_back = lax.all_gather(kv_weight, "blk", axis=0, tiled=True)
     grad_weight = lax.psum_scatter(

time: 540 us -> 519 us (0.961)
  waiting for transfers between devices: 113 us -> 84.7 us
    all_gather x1 -> x0, waiting for transfers between devices: 51.4 us -> none  [shards(): grad_kv = lax.all_gather(grad_own, 'seq', axis=0, tiled=True)]
    all_to_all x0 -> x1, waiting for transfers between devices: none -> 22.8 us  [shards(): lax.all_to_all(jnp.stack([grad_own] * lax.axis_size('seq')), 'seq', 0, 0)]
where the time goes in v1:
time: 519 us; the launch traced here: 513 us
  blocking collectives  229 us (44%)
  waiting for transfers between devices  84.7 us (16%)
  local copies, waits for them, and re-layouts  74 us (14%)
  matrix products  69.1 us (13%)
  other arithmetic  32.9 us (6%)
  between operations  14.2 us (3%)
  starting transfers between devices  9.2 us (2%)
    all_to_all x2, blocking collectives, sum_at_owner(): lax.all_to_all(cut_along(shard, dim, length), axis, 0, 0, tiled=True)  106 us
    psum x1, blocking collectives, shards(): grad_gain = lax.psum(jnp.sum(grad_norm * scaled, axis=0), ('blk', 'seq'))  67.3 us
    unnamed x29, local copies, waits for them, and re-layouts  38.6 us
    all_to_all x1, blocking collectives, shards(): lax.all_to_all(split_cols, 'seq', split_axis=2, concat_axis=0, tiled=True)  38.3 us
    all_gather x1, waiting for transfers between devices, shards(): kv_piece = lax.all_gather(kv_own, 'seq', axis=0, tiled=True)  30.2 us
    all_to_all x1, waiting for transfers between devices, shards(): lax.all_to_all(jnp.stack([grad_own] * lax.axis_size('seq')), 'seq', 0, 0)  22.8 us
    all_to_all x1, waiting for transfers between devices, shards(): lax.all_to_all(grad_cols, 'seq', split_axis=0, concat_axis=2, tiled=True)  22.7 us
    all_gather x1, blocking collectives, shards(): doc_piece = lax.all_gather(query_doc, 'seq', axis=0, tiled=True)  17.1 us
  transfers between devices with their start and end apart: 5, of which 4 were waited for; matrix products, arithmetic and copies ran while one was open for 15% of the time, Pallas kernels for 0%

profile of v1, /device:TPU:1, one launch (start us, length us, event | category | flops | bytes accessed | tf_op | source)
XLA Modules:
  0.0 512.8 jit_solution(5501305438793525802)
XLA Ops:
  8.0 3.2 copy.151
  17.7 38.3 %all_to_all.39 = bf16[128,16,8,64]{0,3,1,2:T(8,128)(2,1)} all-to-all(bf16[128,16,8,64]{0,3,1,2:T(8,128)(2,1)S(1)} %copy.152), channel_id=1, replica_groups=mesh['blk'=16,'seq'=8] {'seq'}, dimensions={2} | all-to-all | bytes 4194304 | tf_op jit(solution)/shard_map/all_to_all | solution.py:42
  56.0 8.3 %all-gather.4.cloned.1.call-done = bf16[1024,1024]{1,0:T(8,128)(2,1)} async-done(((bf16[64,1024]{1,0:T(8,128)(2,1)}), bf16[1024,1024]{1,0:T(8,128)(2,1)}) %all-gather.4.cloned.1.call-update) | async-done | bytes 2097168 | tf_op jit(solution)/shard_map/all_gather | solution.py:45
  64.3 4.6 fusion.22
  68.9 55.1 %all_to_all.40 = f32[8,128,1024]{2,1,0:T(8,128)} all-to-all(f32[8,128,1024]{2,1,0:T(8,128)S(1)} %fusion.22), channel_id=1, replica_groups=mesh['blk'=16,'seq'=8] {'seq'}, dimensions={0} | all-to-all | bytes 8388608 | tf_op jit(solution)/shard_map/all_to_all | solution.py:18
  124.1 3.4 reduce_sum.66
  131.0 17.1 %all-gather = s32[1,1024]{1,0:T(1,128)S(1)} all-gather(s32[1,128]{1,0:T(1,128)S(1)} %copy-done.8), channel_id=2, replica_groups=mesh['blk'=16,'seq'=8] {'seq'}, dimensions={1}, use_global_device_ids=true | all-gather | bytes 4608 | tf_op jit(solution)/shard_map/all_gather | solution.py:70
  148.3 30.2 %all-gather.6.cloned.1.call-done = bf16[1024,1024]{1,0:T(8,128)(2,1)} async-done(((bf16[128,1024]{1,0:T(8,128)(2,1)}), bf16[1024,1024]{1,0:T(8,128)(2,1)}) %all-gather.6.cloned.1.call-update) | async-done | bytes 2097168 | tf_op jit(solution)/shard_map/all_gather | solution.py:69
  183.0 9.1 %fusion.33 = (f32[4,8,128]{2,1,0:T(8,128)S(1)}, f32[4,8,128,1024]{2,3,1,0:T(8,128)}) fusion(bf16[1024,4,128,1]{0,2,3,1:T(8,128)(2,1)S(1)} %bitcast.123, bf16[128,4,8,128]{3,2,1,0:T(8,128)(2,1)} %bitcast.125, pred[128,1024]{0,1:T(8,128)(4,1)S(1)} %fusion.29), kind=kOutput, calls=%fused_computation.52 | convolution fusion | flops 1086320640 | bytes 19021824 | tf_op jit(solution)/shard_map/qgjd,kgd->gjqk/dot_general | solution.py:55
  194.4 8.7 %fusion.1 = f32[4,8,128]{2,1,0:T(8,128)S(1)} fusion(f32[4,8,128,1024]{2,3,1,0:T(8,128)} %get-tuple-element.45, f32[4,8,128]{2,1,0:T(8,128)S(1)} %broadcast_maximum_fusion, pred[128,1024]{0,1:T(8,128)(4,1)S(1)} %fusion.29), kind=kLoop, calls=%fused_computation.5 | loop fusion | flops 12578816 | bytes 16941056 | tf_op jit(solution)/shard_map/reduce_sum | solution.py:78
  203.1 9.9 %fusion.21 = (bf16[128,4,8,128]{0,3,2,1:T(8,128)(2,1)}, f32[4,8,128,128]{2,3,1,0:T(8,128)S(1)}) fusion(f32[128,4,8]{0,2,1:T(8,128)S(1)} %bitcast.141, bf16[1024,4,128,1]{0,2,3,1:T(8,128)(2,1)S(1)} %bitcast.139, f32[4,8,128,1024]{2,3,1,0:T(8,128)} %get-tuple-element.45, f32[4,8,128]{2,1,0:T(8,128)S(1)} %broadcast_maximum_fusion, ...), kind=kOutput, calls=%fused_computation.32 | convolution fusion | flops 1087373312 | bytes 21135360 | tf_op jit(solution)/shard_map/gjqk,kgd->gjqd/dot_general | solution.py:77
  213.4 9.5 %fusion.24 = f32[1024,4,128]{2,0,1:T(8,128)} fusion(bf16[4,8,128,128]{2,3,1,0:T(8,128)(2,1)S(1)} %bitcast.132, f32[4,8,128,1024]{2,3,1,0:T(8,128)} %get-tuple-element.45, f32[4,8,128]{2,1,0:T(8,128)S(1)} %log_add_fusion, pred[128,1024]{0,1:T(8,128)(4,1)S(1)} %fusion.29), kind=kOutput, calls=%fused_computation.39 | convolution fusion | flops 1086324736 | bytes 20070400 | tf_op jit(solution)/shard_map/gjqk,gjqd->kgd/dot_general | solution.py:96
  222.9 10.9 %fusion = bf16[4,8,128,1024]{2,3,1,0:T(8,128)(2,1)} fusion(f32[4,8,128,1024]{2,3,1,0:T(8,128)} %get-tuple-element.45, bf16[1024,4,128,1]{0,2,3,1:T(8,128)(2,1)S(1)} %bitcast.140, bf16[4,8,128,128]{2,3,1,0:T(8,128)(2,1)S(1)} %bitcast.133, f32[4,8,128]{2,1,0:T(8,128)S(1)} %multiply_reduce_fusion.3, f32[4,8,128]{2,1,0:T(8,128)S(1)} %log_add_fusion, ...), kind=kOutput, calls=%fused_computation.1 | convolution fusion | flops 1094713344 | bytes 27426816 | tf_op jit(solution)/shard_map/gjqd,kgd->gjqk/dot_general | solution.py:93
  236.7 3.5 copy.198
  240.1 7.1 %fusion.20 = f32[1024,4,128]{2,0,1:T(8,128)} fusion(bf16[4,8,128,1024]{2,3,1,0:T(8,128)(2,1)} %fusion, bf16[128,4,8,128]{3,2,1,0:T(8,128)(2,1)S(1)} %bitcast.126), kind=kOutput, calls=%fused_computation.30 | convolution fusion | flops 1074266112 | bytes 11534336 | tf_op jit(solution)/shard_map/gjqk,qgjd->kgd/dot_general | solution.py:98
  253.4 50.9 %all_to_all.41 = f32[8,128,1024]{1,2,0:T(8,128)} all-to-all(f32[8,128,1024]{1,2,0:T(8,128)S(1)} %copy.167), channel_id=1, replica_groups=mesh['blk'=16,'seq'=8] {'seq'}, dimensions={0} | all-to-all | bytes 8388608 | tf_op jit(solution)/shard_map/all_to_all | solution.py:18
  310.2 4.3 all-to-all-start.3
  314.7 4.7 copy.175
  319.4 22.8 %all-to-all-done.3 = bf16[8,128,1024]{2,1,0:T(8,128)(2,1)} async-done(((bf16[8,128,1024]{2,1,0:T(8,128)(2,1)}), bf16[8,128,1024]{2,1,0:T(8,128)(2,1)}, u32[]{:S(2)}, u32[]{:S(2)}) %all-to-all-start.3) | async-done | bytes 2097184 | tf_op jit(solution)/shard_map/all_to_all | solution.py:112
  342.2 6.5 %fusion.17 = f32[1024,1024]{1,0:T(8,128)} fusion(bf16[1024,1024]{1,0:T(8,128)(2,1)} %bitcast.31, bf16[128,8,8,128]{3,2,1,0:T(8,128)(2,1)} %bitcast.136), kind=kOutput, calls=%fused_computation.26 | convolution fusion | flops 2147483648 | bytes 8388608 | tf_op jit(solution)/shard_map/dot_general | solution.py:117
  348.7 5.9 %convolution_convert_fusion = bf16[1024,1024]{0,1:T(8,128)(2,1)} fusion(bf16[1024,1024]{1,0:T(8,128)(2,1)} %bitcast.31, bf16[1024,1024]{1,0:T(8,128)(2,1)} %all-gather.4.cloned.1.call-done), kind=kOutput, calls=%fused_computation.38 | convolution fusion | flops 2148532224 | bytes 6291456 | tf_op jit(solution)/shard_map/dot_general | solution.py:122
  354.6 6.2 %copy.170 = bf16[1024,16,1,64]{3,1,2,0:T(8,128)(2,1)} copy(bf16[1024,16,1,64]{0,3,1,2:T(8,128)(2,1)} %bitcast.135) | data formatting | bytes 4194304 | tf_op jit(solution)/shard_map/reshape | solution.py:125
  360.8 7.6 %reshape.229 = bf16[8,2,65536]{2,1,0:T(2,128)(2,1)} reshape(bf16[1024,1,16,64]{3,2,1,0:T(8,128)(2,1)} %bitcast.120) | data formatting | bytes 4194304
  368.4 4.6 all-to-all-start.4
  376.3 5.7 %multiply_convert_fusion.1 = bf16[4,128,8,128]{3,1,2,0:T(8,128)(2,1)} fusion(bf16[1024,4,128,1]{0,2,3,1:T(8,128)(2,1)S(1)} %bitcast.124, bf16[4,8,128,1024]{2,3,1,0:T(8,128)(2,1)} %fusion), kind=kOutput, calls=%fused_computation.35 | convolution fusion | flops 1074790400 | bytes 10485760 | tf_op jit(solution)/shard_map/gjqk,kgd->qgjd/dot_general | solution.py:102
  384.2 22.7 %all-to-all-done.4 = bf16[8,2,65536]{2,1,0:T(2,128)(2,1)} async-done(((bf16[8,2,65536]{2,1,0:T(2,128)(2,1)}), bf16[8,2,65536]{2,1,0:T(2,128)(2,1)}, u32[]{:S(2)}, u32[]{:S(2)}) %all-to-all-start.4) | async-done | bytes 2097184 | tf_op jit(solution)/shard_map/all_to_all | solution.py:126
  406.9 7.4 %reshape.230 = bf16[1024,1,16,64]{3,2,1,0:T(8,128)(2,1)} reshape(bf16[8,2,65536]{2,1,0:T(2,128)(2,1)} %all-to-all-done.4) | data formatting | bytes 4194304
  414.3 5.5 %copy.171 = bf16[1024,16,1,64]{0,3,2,1:T(8,128)(2,1)} copy(bf16[1024,16,1,64]{3,1,2,0:T(8,128)(2,1)} %bitcast.121) | data formatting | bytes 4194304 | tf_op jit(solution)/shard_map/all_to_all | solution.py:126
  425.2 4.8 multiply_reduce_fusion
  430.0 4.4 fusion.16
  434.4 4.1 copy.179
  438.7 67.3 %psum.7 = f32[8192]{0:T(1024)} all-reduce(f32[8192]{0:T(1024)S(1)} %reduce_sum.72), channel_id=1, replica_groups=mesh['blk'=16,'seq'=8] {'blk','seq'}, use_global_device_ids=true, to_apply=%region_9.10 | all-reduce | flops 8192 | bytes 65536 | tf_op jit(solution)/shard_map/psum | solution.py:130
  (58 shorter events, 44.5 us)
Async XLA Ops:
  7.2 57.1 %all-gather.4.cloned.1.call-start = ((), (), s32[]{:S(2)}) async-start(), calls=%async_computation.6 | async-start | bytes 2228224 | tf_op jit(solution)/shard_map/all_gather | solution.py:45
  7.9 5.5 %copy-start.7 = (f32[8192]{0:T(1024)S(1)}, f32[8192]{0:T(1024)}, u32[]{:S(2)}) copy-start(f32[8192]{0:T(1024)} %param.11) | copy-start | bytes 98308
  7.9 170.6 %all-gather.6.cloned.1.call-start = ((), (), s32[]{:S(2)}) async-start(), calls=%async_computation.7 | async-start | bytes 2359296 | tf_op jit(solution)/shard_map/all_gather | solution.py:69
  124.0 3.5 copy-start.5
  124.0 6.9 %copy-start.8 = (s32[1,128]{1,0:T(1,128)S(1)}, s32[1,128]{1,0:T(1,128)}, u32[]{:S(2)}) copy-start(s32[1,128]{1,0:T(1,128)} %param.9) | copy-start | bytes 1540
  194.4 8.7 %copy-start.6 = (bf16[1024,512]{0,1:T(8,128)(2,1)S(1)}, bf16[1024,512]{0,1:T(8,128)(2,1)}, u32[]{:S(2)}) copy-start(bf16[1024,512]{0,1:T(8,128)(2,1)} %copy.157) | copy-start | bytes 3145732
  203.1 9.9 %copy-start.3 = (bf16[1,128,4096]{1,2,0:T(8,128)(2,1)S(1)}, bf16[1,128,4096]{1,2,0:T(8,128)(2,1)}, u32[]{:S(2)}) copy-start(bf16[1,128,4096]{1,2,0:T(8,128)(2,1)} %copy.159) | copy-start | bytes 3145732
  236.7 3.5 copy-start.1
  250.1 2.2 copy-start.2
  310.2 32.0 %all-to-all-start.3 = ((bf16[8,128,1024]{2,1,0:T(8,128)(2,1)}), bf16[8,128,1024]{2,1,0:T(8,128)(2,1)}, u32[]{:S(2)}, u32[]{:S(2)}) async-start(bf16[8,128,1024]{2,1,0:T(8,128)(2,1)} %stack.2), calls=%async_computation.3 | async-start | bytes 4194304 | tf_op jit(solution)/shard_map/all_to_all | solution.py:112
  314.5 191.5 %reduce-scatter.2.cloned.1.call-start = ((), (), s32[]{:S(2)}) async-start(), calls=%async_computation.8 | async-start | bytes 4456448 | tf_op jit(solution)/shard_map/reduce_scatter | solution.py:116
  368.4 38.6 %all-to-all-start.4 = ((bf16[8,2,65536]{2,1,0:T(2,128)(2,1)}), bf16[8,2,65536]{2,1,0:T(2,128)(2,1)}, u32[]{:S(2)}, u32[]{:S(2)}) async-start(bf16[8,2,65536]{2,1,0:T(2,128)(2,1)} %reshape.229), calls=%async_computation.4 | async-start | bytes 4194304 | tf_op jit(solution)/shard_map/all_to_all | solution.py:126
  422.9 2.2 copy-start
  422.9 2.3 copy-start.4
Sparse Core Ops, SparseCore 0:
  9.7 54.5 all-gather.3
  127.6 50.8 all-gather.5
  348.8 70.4 reduce-scatter.1
